TPU v7x, 32 devices: a whole 2x2x4 slice. The times are simulated.
32 devices in a mesh: ia: 4 (over y, x), ja: 4 (over z), col: 2 (over core).
Axes of the slice: x: 2, y: 2, z: 4, core: 2. Of those that a mesh axis runs over, the one named last changes fastest.
Arguments:
- pair_rep: bfloat16 [512, 512, 128], P('ia', 'ja'), may hold values from -6 to 6
- norm_gain: float32 [128], replicated, may hold values from 0.1 to 1.9
- weights: bfloat16 [4, 128, 128], P(None, None, 'col'), may hold values from -0.5 to 0.5
- residue_mask: int32 [512], replicated, may hold values 0 or 1
- product_grad: bfloat16 [512, 128, 512], P('ia', 'col', 'ja'), may hold values from -1 to 1
Outputs:
- pair_grad: bfloat16 [512, 512, 128], P('ia', 'ja')
- weight_grads: float32 [4, 128, 128], P(None, None, 'col')
All inputs are finite; a program needn't handle non-finite values.
Results may differ from a plain program's by a relative error of at most 0.0067.
Values may be sent and summed in bfloat16 or wider, within the bound.
A program may use at most 128 MiB of HBM per device.

v0:
```python
import jax
import jax.numpy as jnp
from jax import lax
from jax.sharding import PartitionSpec as P

CLIP_LIMIT = 64.0


def gate_terms(incoming, linear, gate_pre, pair_valid):
    sigmoid_gate = jax.nn.sigmoid(gate_pre)
    through = incoming * pair_valid
    return (through * sigmoid_gate, through * linear * sigmoid_gate * (1.0 - sigmoid_gate))


def on_device(pair_rep, norm_gain, weights, residue_mask, product_grad):
    row_count = pair_rep.shape[0]
    col_count = pair_rep.shape[1]
    row_first = lax.axis_index("ia") * row_count
    col_first = lax.axis_index("ja") * col_count
    validity = residue_mask.astype(jnp.float32)
    row_valid = lax.dynamic_slice_in_dim(validity, row_first, row_count)
    col_valid = lax.dynamic_slice_in_dim(validity, col_first, col_count)
    pair_valid = row_valid[:, None, None] * col_valid[None, None, :]
    floats = pair_rep.astype(jnp.float32)
    centred = floats - jnp.mean(floats, axis=-1, keepdims=True)
    inv_std = lax.rsqrt(jnp.mean(centred * centred, axis=-1, keepdims=True) + 1e-05)
    unit_rows = centred * inv_std
    normed = (unit_rows * norm_gain).astype(jnp.bfloat16)
    projected = jnp.einsum("ikd,wdc->wick", normed, weights, preferred_element_type=jnp.float32)
    left_side = (pair_valid * jax.nn.sigmoid(projected[1]) * projected[0]).astype(jnp.bfloat16)
    right_side = (pair_valid * jax.nn.sigmoid(projected[3]) * projected[2]).astype(jnp.bfloat16)
    row_panel = lax.all_gather(product_grad, "ja", axis=2, tiled=True)
    panel_part = row_panel
    grad_left = jnp.einsum(
        "icj,jck->ick",
        panel_part,
        lax.all_gather(right_side, "ia", axis=0, tiled=True),
        preferred_element_type=jnp.float32,
    )
    panel_part = row_panel
    grad_right = lax.psum_scatter(
        jnp.einsum("icj,ick->jck", panel_part, left_side, preferred_element_type=jnp.float32),
        "ia",
        scatter_dimension=0,
        tiled=True,
    )
    lin_a, gate_a = gate_terms(grad_left, projected[0], projected[1], pair_valid)
    lin_b, gate_b = gate_terms(grad_right, projected[2], projected[3], pair_valid)
    proj_grads = jnp.stack([lin_a, gate_a, lin_b, gate_b]).astype(jnp.bfloat16)
    grad_part = jnp.einsum("ikd,wick->wdc", normed, proj_grads, preferred_element_type=jnp.float32)
    input_part = jnp.einsum(
        "wick,wdc->ikd", proj_grads, weights, preferred_element_type=jnp.float32
    )
    normed_grad = lax.psum(input_part, "col")
    scaled = normed_grad * norm_gain
    pair_grad = inv_std * (
        scaled
        - jnp.mean(scaled, axis=-1, keepdims=True)
        - unit_rows * jnp.mean(scaled * unit_rows, axis=-1, keepdims=True)
    )
    summed = lax.psum(grad_part, ("ia", "ja"))
    squares = lax.psum(jnp.sum(summed * summed), "col")
    factor = jnp.minimum(1.0, CLIP_LIMIT * lax.rsqrt(squares + 1e-06))
    weight_grads = summed * factor
    return (pair_grad.astype(jnp.bfloat16), weight_grads)


def solution(mesh):
    placed = (P("ia", "ja", None), P(), P(None, None, "col"), P(), P("ia", "col", "ja"))
    return jax.shard_map(
        on_device,
        mesh=mesh,
        in_specs=placed,
        out_specs=(P("ia", "ja", None), P(None, None, "col")),
        check_vma=False,
    )
```

profile of v0, /device:TPU:0, one launch (start us, length us, event | category | flops | bytes accessed | tf_op | source)
XLA Modules:
  0.0 660.3 jit_solution(14896707460684824877)
XLA Ops:
  7.2 0.0 copy-start
  7.2 0.0 copy-start.10
  7.2 0.0 all-gather.5.cloned.1.call-start
  7.2 4.3 copy.18
  11.5 0.0 all-gather.5.cloned.1.call-update
  11.5 0.0 all-gather.3.cloned.1.call-start
  11.6 0.0 copy-done.10
  11.6 0.0 copy-start.2
  11.6 0.1 fusion.41
  11.7 0.1 broadcast_multiply_fusion.1
  11.8 0.0 copy-start.9
  11.8 3.5 convert_reduce_fusion
  15.3 0.0 copy-done.2
  15.3 4.8 fusion.10
  20.1 0.0 copy-done
  20.2 0.0 copy-done.9
  20.2 4.7 convolution_bitcast_fusion
  24.9 0.0 copy-start.1
  24.9 5.9 copy-done.1
  30.8 2.6 multiply_convert_fusion.5
  33.4 0.0 all-gather.3.cloned.1.call-update
  33.4 0.5 reduce-scatter.2.cloned.1.call-start
  33.9 129.6 %all-gather.5.cloned.1.call-done = bf16[128,64,512]{2,0,1:T(8,128)(2,1)} async-done(((bf16[128,64,128]{2,0,1:T(8,128)(2,1)}), bf16[128,64,512]{2,0,1:T(8,128)(2,1)}) %all-gather.5.cloned.1.call-update) | async-done | bytes 8388624 | tf_op jit(solution)/shard_map/all_gather | solution.py:32
  163.5 87.5 %all-gather.3.cloned.1.call-done = bf16[512,64,128]{2,1,0:T(8,128)(2,1)} async-done(((bf16[128,64,128]{2,1,0:T(8,128)(2,1)}), bf16[512,64,128]{2,1,0:T(8,128)(2,1)}) %all-gather.3.cloned.1.call-update) | async-done | bytes 8388624 | tf_op jit(solution)/shard_map/all_gather | solution.py:37
  251.0 25.2 %fusion.11 = f32[64,128,128]{2,1,0:T(8,128)} fusion(bf16[128,64,512]{2,0,1:T(8,128)(2,1)} %all-gather.5.cloned.1.call-done, bf16[512,64,128]{2,1,0:T(8,128)(2,1)} %all-gather.3.cloned.1.call-done), kind=kOutput, calls=%fused_computation.15 | convolution fusion | flops 1073741824 | bytes 20971520 | tf_op jit(solution)/shard_map/icj,jck->ick/dot_general | solution.py:34
  276.2 5.4 copy.20
  281.6 6.8 %fusion.28 = (bf16[1,128,64,128]{3,2,1,0:T(8,128)(2,1)S(1)}, bf16[1,128,64,128]{3,2,1,0:T(8,128)(2,1)}, bf16[128,64,128]{2,1,0:T(8,128)(2,1)S(1)}) fusion(f32[64,128,128]{1,0,2:T(8,128)} %copy.20, f32[128,128]{1,0:T(8,128)S(1)} %broadcast_multiply_fusion.1, f32[4,128,64,128]{3,2,0,1:T(8,128)} %copy-done.1), kind=kLoop, calls=%fused_computation.43 | loop fusion | flops 14680064 | bytes 18939904 | tf_op jit(solution)/shard_map/stack | solution.py:49
  288.5 14.1 %fusion.32 = f32[64,128,512]{2,1,0:T(8,128)} fusion(bf16[128,64,512]{2,0,1:T(8,128)(2,1)} %all-gather.5.cloned.1.call-done, bf16[128,64,128]{2,1,0:T(8,128)(2,1)S(1)} %get-tuple-element.8), kind=kOutput, calls=%fused_computation.47 | convolution fusion | flops 1073741824 | bytes 27262976 | tf_op jit(solution)/shard_map/icj,ick->jck/dot_general | solution.py:42
  302.6 16.6 %copy.23 = f32[64,128,512]{1,0,2:T(8,128)} copy(f32[64,128,512]{2,1,0:T(8,128)} %fusion.32) | data formatting | bytes 33554432 | tf_op jit(solution)/shard_map/icj,ick->jck/dot_general | solution.py:42
  319.2 0.0 reduce-scatter.2.cloned.1.call-update
  319.2 0.0 all-reduce.5.cloned.1.call-start
  319.2 153.8 %reduce-scatter.2.cloned.1.call-done = f32[128,64,128]{2,1,0:T(8,128)} async-done(((f32[512,64,128]{2,1,0:T(8,128)}), f32[128,64,128]{2,1,0:T(8,128)}) %reduce-scatter.2.cloned.1.call-update) | async-done | bytes 4194320 | tf_op jit(solution)/shard_map/reduce_scatter | solution.py:41
  473.1 0.0 copy-start.3
  473.1 0.0 copy-start.6
  473.1 6.0 fusion.30
  479.1 0.0 copy-start.7
  479.1 0.0 copy-start.8
  479.2 1.3 copy-done.7
  480.4 0.7 copy-done.8
  481.1 0.0 copy-done.3
  481.1 0.0 copy-done.6
  481.1 5.4 fusion.34
  486.5 0.0 all-reduce.5.cloned.1.call-update
  486.6 0.0 all-reduce.3.cloned.1.call-start
  486.6 6.5 convolution_bitcast_fusion.1
  493.1 0.0 all-reduce.3.cloned.1.call-update
  493.1 99.0 %all-reduce.5.cloned.1.call-done = f32[4,128,64]{1,2,0:T(8,128)} async-done(((f32[4,128,64]{1,2,0:T(8,128)}), f32[4,128,64]{1,2,0:T(8,128)}) %all-reduce.5.cloned.1.call-update) | async-done | bytes 131088 | tf_op jit(solution)/shard_map/psum | solution.py:61
  592.1 1.5 multiply_reduce_fusion.1
  593.7 3.1 psum.23
  597.4 1.6 broadcast_multiply_fusion
  599.0 32.2 %all-reduce.3.cloned.1.call-done = f32[128,128,128]{2,1,0:T(8,128)} async-done(((f32[128,128,128]{2,1,0:T(8,128)}), f32[128,128,128]{2,1,0:T(8,128)}) %all-reduce.3.cloned.1.call-update) | async-done | bytes 8388624 | tf_op jit(solution)/shard_map/psum | solution.py:54
  631.2 0.0 copy-start.4
  631.2 0.0 copy-start.5
  631.2 11.6 %multiply_reduce_fusion = (f32[128,128]{1,0:T(8,128)S(1)}, f32[128,128]{1,0:T(8,128)S(1)}) fusion(f32[128,128,128]{2,1,0:T(8,128)} %all-reduce.3.cloned.1.call-done, f32[128]{0:T(128)S(1)} %copy-done.9, f32[128,128]{1,0:T(8,128)S(1)} %add_rsqrt_fusion, f32[128,128]{1,0:T(8,128)S(1)} %broadcast_multiply_fusion.4, bf16[128,128,128]{2,1,0:T(8,128)(2,1)} %param.5), kind=kLoop, calls=%fused_computation.17 | loop fusion | flops 14647296 | bytes 12845568 | tf_op jit(solution)/shard_map/reduce_sum | solution.py:58
  642.8 0.0 copy-done.4
  642.8 0.0 copy-done.5
  642.8 10.7 %fusion.9 = bf16[128,128,128]{2,1,0:T(8,128)(2,1)} fusion(bf16[128,128,128]{2,1,0:T(8,128)(2,1)S(1)} %copy-done.4, f32[128,128,128]{2,1,0:T(8,128)S(1)} %copy-done.5, f32[128,128]{1,0:T(8,128)S(1)} %get-tuple-element.11, f32[128,128]{1,0:T(8,128)S(1)} %get-tuple-element.12, f32[128]{0:T(128)S(1)} %copy-done.9, f32[128,128]{1,0:T(8,128)S(1)} %add_rsqrt_fusion, ...), kind=kLoop, calls=%fused_computation.12 | loop fusion | flops 18874368 | bytes 17039872 | tf_op jit(solution)/shard_map/convert_element_type | solution.py:65
  (4 shorter events, 0.0 us)
Async XLA Ops:
  7.2 13.0 %copy-start = (bf16[4,128,64]{1,2,0:T(8,128)(2,1)S(1)}, bf16[4,128,64]{1,2,0:T(8,128)(2,1)}, u32[]{:S(2)}) copy-start(bf16[4,128,64]{1,2,0:T(8,128)(2,1)} %param.7) | copy-start | bytes 196612
  7.2 4.4 copy-start.10
  7.2 156.3 %all-gather.5.cloned.1.call-start = ((), (), s32[]{:S(2)}) async-start(), calls=%async_computation.2 | async-start | bytes 10485760 | tf_op jit(solution)/shard_map/all_gather | solution.py:32
  11.5 239.5 %all-gather.3.cloned.1.call-start = ((), (), s32[]{:S(2)}) async-start(), calls=%async_computation.1 | async-start | bytes 10485760 | tf_op jit(solution)/shard_map/all_gather | solution.py:37
  11.6 3.7 copy-start.2
  11.8 8.4 %copy-start.9 = (f32[128]{0:T(128)S(1)}, f32[128]{0:T(128)}, u32[]{:S(2)}) copy-start(f32[128]{0:T(128)} %param.6) | copy-start | bytes 1540
  24.9 5.9 copy-start.1
  33.4 439.6 %reduce-scatter.2.cloned.1.call-start = ((), (), s32[]{:S(2)}) async-start(), calls=%async_computation.3 | async-start | bytes 20971520 | tf_op jit(solution)/shard_map/reduce_scatter | solution.py:41
  319.2 272.9 %all-reduce.5.cloned.1.call-start = ((), (), s32[]{:S(2)}) async-start(), calls=%async_computation.5 | async-start | bytes 262144 | tf_op jit(solution)/shard_map/psum | solution.py:61
  473.1 8.0 %copy-start.3 = (bf16[128,128,128]{2,1,0:T(8,128)(2,1)S(1)}, bf16[128,128,128]{2,1,0:T(8,128)(2,1)}, u32[]{:S(2)}) copy-start(bf16[128,128,128]{2,1,0:T(8,128)(2,1)} %param.5) | copy-start | bytes 12582916
  473.1 8.0 %copy-start.6 = (bf16[1,128,64,128]{3,2,1,0:T(8,128)(2,1)S(1)}, bf16[1,128,64,128]{3,2,1,0:T(8,128)(2,1)}, u32[]{:S(2)}) copy-start(bf16[1,128,64,128]{3,2,1,0:T(8,128)(2,1)} %get-tuple-element.5) | copy-start | bytes 6291460
  479.1 1.3 copy-start.7
  479.1 2.0 copy-start.8
  486.6 144.6 %all-reduce.3.cloned.1.call-start = ((), (), s32[]{:S(2)}) async-start(), calls=%async_computation.4 | async-start | bytes 16777216 | tf_op jit(solution)/shard_map/psum | solution.py:54
  631.2 11.6 %copy-start.4 = (bf16[128,128,128]{2,1,0:T(8,128)(2,1)S(1)}, bf16[128,128,128]{2,1,0:T(8,128)(2,1)}, u32[]{:S(2)}) copy-start(bf16[128,128,128]{2,1,0:T(8,128)(2,1)} %param.5) | copy-start | bytes 12582916
  631.2 11.6 %copy-start.5 = (f32[128,128,128]{2,1,0:T(8,128)S(1)}, f32[128,128,128]{2,1,0:T(8,128)}, u32[]{:S(2)}) copy-start(f32[128,128,128]{2,1,0:T(8,128)} %all-reduce.3.cloned.1.call-done) | copy-start | bytes 25165828
Sparse Core Ops, SparseCore 0:
  11.6 151.8 all-gather.4
  165.4 85.6 all-gather.2
  319.3 153.7 reduce-scatter.1
  486.7 105.3 all-reduce.4
  594.4 36.6 all-reduce.2
where the time goes:
time: 668 us; the launch traced here: 660 us
  waiting for transfers between devices  502 us (75%)
  matrix products  55.9 us (8%)
  other arithmetic  49.3 us (7%)
  local copies, waits for them, and re-layouts  34.2 us (5%)
  between operations  14.9 us (2%)
    reduce_scatter x1, waiting for transfers between devices, on_device(): lax.psum_scatter(jnp.einsum('icj,ick->jck', panel_part, left_side, prefer...  154 us
    all_gather x1, waiting for transfers between devices, on_device(): row_panel = lax.all_gather(product_grad, 'ja', axis=2, tiled=True)  130 us
    psum x1, waiting for transfers between devices, on_device(): summed = lax.psum(grad_part, ('ia', 'ja'))  99 us
    all_gather x1, waiting for transfers between devices, on_device(): lax.all_gather(right_side, 'ia', axis=0, tiled=True)  87.5 us
    psum x1, waiting for transfers between devices, on_device(): normed_grad = lax.psum(input_part, 'col')  32.2 us
    dot_general x1, matrix products, on_device(): jnp.einsum('icj,jck->ick', panel_part, lax.all_gather(right_side, 'ia', a...  25.2 us
    dot_general x1, local copies, waits for them, and re-layouts, on_device(): jnp.einsum('icj,ick->jck', panel_part, left_side, preferred_element_type=...  16.6 us
    dot_general x1, matrix products, on_device(): jnp.einsum('icj,ick->jck', panel_part, left_side, preferred_element_type=...  14.1 us
  transfers between devices with their start and end apart: 5, of which 5 were waited for; matrix products, arithmetic and copies ran while one was open for 4% of the time, Pallas kernels for 0%

commit v1 on v0

--- a/solution.py
+++ b/solution.py
@@ -31,12 +31,27 @@
     right_side = (pair_valid * jax.nn.sigmoid(projected[3]) * projected[2]).astype(jnp.bfloat16)
     row_panel = lax.all_gather(product_grad, "ja", axis=2, tiled=True)
     panel_part = row_panel
-    grad_left = jnp.einsum(
+    peers, mine = (lax.axis_size("ia"), lax.axis_index("ia"))
+    left = [(i, (i - 1) % peers) for i in range(peers)]
+    rows = right_side.shape[0]
+    held = right_side
+    total = jnp.einsum(
         "icj,jck->ick",
-        panel_part,
-        lax.all_gather(right_side, "ia", axis=0, tiled=True),
+        lax.dynamic_slice_in_dim(panel_part, mine * rows, held.shape[0], axis=2),
+        held,
         preferred_element_type=jnp.float32,
     )
+    for hop in range(1, peers):
+        held = lax.ppermute(held, "ia", left)
+        total = total + jnp.einsum(
+            "icj,jck->ick",
+            lax.dynamic_slice_in_dim(
+                panel_part, (mine + hop) % peers * rows, held.shape[0], axis=2
+            ),
+            held,
+            preferred_element_type=jnp.float32,
+        )
+    grad_left = total
     panel_part = row_panel
     grad_right = lax.psum_scatter(
         jnp.einsum("icj,ick->jck", panel_part, left_side, preferred_element_type=jnp.float32),

time: 668 us -> 623 us (0.933)
  waiting for transfers between devices: 502 us -> 419 us
  local copies, waits for them, and re-layouts: 34.2 us -> 52.5 us
  starting transfers between devices: 0.67 us -> 11.4 us
  other arithmetic: 49.3 us -> 57.8 us
    ppermute x0 -> x3, waiting for transfers between devices: none -> 132 us  [on_device(): held = lax.ppermute(held, 'ia', left)]
    all_gather x1, waiting for transfers between devices: 130 us -> 0.01 us  [on_device(): row_panel = lax.all_gather(product_grad, 'ja', axis=2, tiled=True)]
    all_gather x1 -> x0, waiting for transfers between devices: 87.5 us -> none  [on_device(): lax.all_gather(right_side, 'ia', axis=0, tiled=True)]
    dot_general x1 -> x4, local copies, waits for them, and re-layouts: 5.42 us -> 21.6 us  [the longest x3 16.2 us: on_device(): jnp.einsum('icj,jck->ick', lax.dynamic_slice_in_dim(panel_part, (mine + h...]
    ppermute x0 -> x3, starting transfers between devices: none -> 11.3 us  [on_device(): held = lax.ppermute(held, 'ia', left)]
    another operation x2, other arithmetic: 12.9 us -> 22.7 us  [on_device(): proj_grads = jnp.stack([lin_a, gate_a, lin_b, gate_b]).astype(jnp.bfloat16)]
    unnamed x23 -> x25, local copies, waits for them, and re-layouts: 12.2 us -> 14.2 us
    dot_general x1 -> x4, matrix products: 25.2 us -> 24.7 us  [the longest x3 19 us: on_device(): jnp.einsum('icj,jck->ick', lax.dynamic_slice_in_dim(panel_part, (mine + h...]
  transfers between devices with their start and end apart: 5 -> 7, of which waited for: 5 -> 6; matrix products, arithmetic and copies ran while one was open for 4% -> 4% of each run, Pallas kernels for 0% -> 0%
where the time goes in v1:
time: 623 us; the launch traced here: 615 us
  waiting for transfers between devices  419 us (67%)
  other arithmetic  57.8 us (9%)
  matrix products  55.7 us (9%)
  local copies, waits for them, and re-layouts  52.5 us (8%)
  between operations  14.9 us (2%)
  starting transfers between devices  11.4 us (2%)
    reduce_scatter x1, waiting for transfers between devices, on_device(): lax.psum_scatter(jnp.einsum('icj,ick->jck', panel_part, left_side, prefer...  156 us
    ppermute x3, waiting for transfers between devices, on_device(): held = lax.ppermute(held, 'ia', left)  132 us
    psum x1, waiting for transfers between devices, on_device(): summed = lax.psum(grad_part, ('ia', 'ja'))  98.7 us
    psum x1, waiting for transfers between devices, on_device(): normed_grad = lax.psum(input_part, 'col')  32.2 us
    another operation x2, other arithmetic, on_device(): proj_grads = jnp.stack([lin_a, gate_a, lin_b, gate_b]).astype(jnp.bfloat16)  22.7 us
    dot_general x3, matrix products, on_device(): jnp.einsum('icj,jck->ick', lax.dynamic_slice_in_dim(panel_part, (mine + h...  19 us
    dot_general x1, local copies, waits for them, and re-layouts, on_device(): jnp.einsum('icj,ick->jck', panel_part, left_side, preferred_element_type=...  16.5 us
    dot_general x3, local copies, waits for them, and re-layouts, on_device(): jnp.einsum('icj,jck->ick', lax.dynamic_slice_in_dim(panel_part, (mine + h...  16.2 us
  transfers between devices with their start and end apart: 7, of which 6 were waited for; matrix products, arithmetic and copies ran while one was open for 4% of the time, Pallas kernels for 0%

profile of v1, /device:TPU:0, one launch (start us, length us, event | category | flops | bytes accessed | tf_op | source)
XLA Modules:
  0.0 614.7 jit_solution(14509186678330371873)
XLA Ops:
  7.2 0.0 copy-start
  7.2 0.0 copy-start.11
  7.2 0.0 all-gather.2.cloned.1.call-start
  7.2 4.3 copy.9
  11.5 0.0 all-gather.2.cloned.1.call-update
  11.5 0.0 reduce-scatter.2.cloned.1.call-start
  11.6 0.0 copy-done.11
  11.6 0.0 copy-start.2
  11.6 0.1 fusion.55
  11.7 0.1 broadcast_multiply_fusion.1
  11.8 0.0 copy-start.10
  11.8 3.5 convert_reduce_fusion
  15.3 0.0 copy-done.2
  15.3 4.8 fusion.10
  20.1 0.0 copy-done
  20.2 0.0 copy-done.10
  20.2 4.7 convolution_bitcast_fusion
  24.9 0.0 copy-start.1
  24.9 5.9 copy-done.1
  30.8 1.3 multiply_convert_fusion.5
  32.1 4.0 collective-permute-start
  36.0 44.9 %collective-permute-done = bf16[128,64,128]{2,1,0:T(8,128)(2,1)S(1)} collective-permute-done((bf16[128,64,128]{2,1,0:T(8,128)(2,1)S(1)}, bf16[128,64,128]{2,1,0:T(8,128)(2,1)S(1)}, u32[]{:S(2)}, u32[]{:S(2)}) %collective-permute-start) | collective-permute-done | bytes 2097184 | tf_op jit(solution)/shard_map/ppermute | solution.py:45
  80.9 0.0 copy-start.6
  80.9 1.4 copy-done.6
  82.3 3.4 collective-permute-start.1
  85.7 44.0 %collective-permute-done.1 = bf16[128,64,128]{2,1,0:T(8,128)(2,1)} collective-permute-done((bf16[128,64,128]{2,1,0:T(8,128)(2,1)S(1)}, bf16[128,64,128]{2,1,0:T(8,128)(2,1)}, u32[]{:S(2)}, u32[]{:S(2)}) %collective-permute-start.1) | collective-permute-done | bytes 2097184 | tf_op jit(solution)/shard_map/ppermute | solution.py:45
  129.7 3.9 collective-permute-start.2
  133.6 43.5 %collective-permute-done.2 = bf16[128,64,128]{2,1,0:T(8,128)(2,1)} collective-permute-done((bf16[128,64,128]{2,1,0:T(8,128)(2,1)}, bf16[128,64,128]{2,1,0:T(8,128)(2,1)}, u32[]{:S(2)}, u32[]{:S(2)}) %collective-permute-start.2) | collective-permute-done | bytes 2097184 | tf_op jit(solution)/shard_map/ppermute | solution.py:45
  177.1 6.3 %fusion.32 = f32[64,128,128]{2,1,0:T(8,128)} fusion(bf16[128,64,128]{2,1,0:T(8,128)(2,1)} %collective-permute-done.2, bf16[128,64,512]{2,0,1:T(8,128)(2,1)} %all-gather.2.cloned.1.call-done, s32[]{:T(128)S(6)} %select_n.38), kind=kOutput, calls=%fused_computation.47 | convolution fusion | flops 268435456 | bytes 8388612 | tf_op jit(solution)/shard_map/icj,jck->ick/dot_general | solution.py:46
  183.4 5.4 copy.17
  188.8 6.3 %fusion.34 = f32[64,128,128]{2,1,0:T(8,128)} fusion(bf16[128,64,128]{2,1,0:T(8,128)(2,1)} %collective-permute-done.1, bf16[128,64,512]{2,0,1:T(8,128)(2,1)} %all-gather.2.cloned.1.call-done, s32[]{:T(128)S(6)} %select_n.36), kind=kOutput, calls=%fused_computation.49 | convolution fusion | flops 268435456 | bytes 8388612 | tf_op jit(solution)/shard_map/icj,jck->ick/dot_general | solution.py:46
  195.2 5.4 copy.15
  200.6 6.3 %fusion.36 = f32[64,128,128]{2,1,0:T(8,128)} fusion(bf16[128,64,128]{2,1,0:T(8,128)(2,1)} %copy-done.6, bf16[128,64,512]{2,0,1:T(8,128)(2,1)} %all-gather.2.cloned.1.call-done, s32[]{:T(128)S(6)} %select_n.34), kind=kOutput, calls=%fused_computation.51 | convolution fusion | flops 268435456 | bytes 8388612 | tf_op jit(solution)/shard_map/icj,jck->ick/dot_general | solution.py:46
  206.9 5.4 copy.13
  212.3 5.7 fusion.38
  218.0 5.4 copy.12
  223.4 12.3 %fusion.26 = (bf16[1,128,64,128]{3,2,1,0:T(8,128)(2,1)S(1)}, f32[128,64,128]{2,1,0:T(8,128)}, bf16[128,64,128]{2,1,0:T(8,128)(2,1)S(1)}) fusion(f32[4,128,64,128]{3,2,0,1:T(8,128)} %copy-done.1, f32[128,128]{1,0:T(8,128)S(1)} %broadcast_multiply_fusion.1, f32[64,128,128]{1,0,2:T(8,128)} %copy.17, f32[64,128,128]{1,0,2:T(8,128)} %copy.15, ...), kind=kLoop, calls=%fused_computation.41 | loop fusion | flops 12582912 | bytes 33619968 | tf_op jit(solution)/shard_map/stack | solution.py:64
  235.7 14.1 %fusion.30 = f32[64,128,512]{2,1,0:T(8,128)} fusion(bf16[128,64,512]{2,0,1:T(8,128)(2,1)} %all-gather.2.cloned.1.call-done, bf16[128,64,128]{2,1,0:T(8,128)(2,1)S(1)} %get-tuple-element.8), kind=kOutput, calls=%fused_computation.45 | convolution fusion | flops 1073741824 | bytes 27262976 | tf_op jit(solution)/shard_map/icj,ick->jck/dot_general | solution.py:57
  249.9 16.5 %copy.20 = f32[64,128,512]{1,0,2:T(8,128)} copy(f32[64,128,512]{2,1,0:T(8,128)} %fusion.30) | data formatting | bytes 33554432 | tf_op jit(solution)/shard_map/icj,ick->jck/dot_general | solution.py:57
  266.4 0.0 reduce-scatter.2.cloned.1.call-update
  266.4 0.0 all-reduce.5.cloned.1.call-start
  266.5 156.0 %reduce-scatter.2.cloned.1.call-done = f32[128,64,128]{2,1,0:T(8,128)} async-done(((f32[512,64,128]{2,1,0:T(8,128)}), f32[128,64,128]{2,1,0:T(8,128)}) %reduce-scatter.2.cloned.1.call-update) | async-done | bytes 4194320 | tf_op jit(solution)/shard_map/reduce_scatter | solution.py:56
  422.5 10.3 %fusion.28 = (bf16[1,128,64,128]{3,2,1,0:T(8,128)(2,1)S(1)}, bf16[1,128,64,128]{3,2,1,0:T(8,128)(2,1)S(1)}, bf16[1,128,64,128]{3,2,1,0:T(8,128)(2,1)S(1)}) fusion(f32[128,64,128]{2,1,0:T(8,128)} %reduce-scatter.2.cloned.1.call-done, f32[128,128]{1,0:T(8,128)S(1)} %broadcast_multiply_fusion.1, f32[4,128,64,128]{3,2,0,1:T(8,128)} %copy-done.1, ...), kind=kLoop, calls=%fused_computation.43 | loop fusion | flops 19922944 | bytes 31522816 | tf_op jit(solution)/shard_map/stack | solution.py:64
  432.8 0.0 copy-start.7
  432.8 0.0 copy-start.8
  432.9 0.0 copy-start.9
  432.9 1.3 copy-done.7
  434.2 0.6 copy-done.8
  434.8 0.7 copy-done.9
  435.5 0.0 copy-done.3
  435.5 5.4 fusion.44
  440.9 0.0 all-reduce.5.cloned.1.call-update
  441.0 0.0 all-reduce.3.cloned.1.call-start
  441.0 6.7 %convolution_bitcast_fusion.1 = f32[128,128,128]{2,1,0:T(8,128)} fusion(bf16[1,128,64,128]{3,2,1,0:T(8,128)(2,1)} %copy-done.8, bf16[1,128,64,128]{3,2,1,0:T(8,128)(2,1)} %copy-done.7, bf16[1,128,64,128]{3,2,1,0:T(8,128)(2,1)} %copy-done.9, bf16[1,128,64,128]{3,2,1,0:T(8,128)(2,1)S(1)} %get-tuple-element.4, bf16[4,128,64]{1,2,0:T(8,128)(2,1)S(1)} %copy-done), kind=kOutput, calls=%fused_computation.40 | convolution fusion | flops 1086324736 | bytes 16842752 | tf_op jit(solution)/shard_map/wick,wdc->ikd/dot_general | solution.py:66
  447.8 0.0 all-reduce.3.cloned.1.call-update
  447.8 98.7 %all-reduce.5.cloned.1.call-done = f32[4,128,64]{1,2,0:T(8,128)} async-done(((f32[4,128,64]{1,2,0:T(8,128)}), f32[4,128,64]{1,2,0:T(8,128)}) %all-reduce.5.cloned.1.call-update) | async-done | bytes 131088 | tf_op jit(solution)/shard_map/psum | solution.py:76
  546.5 1.5 multiply_reduce_fusion.1
  548.1 3.1 psum.23
  551.8 1.6 broadcast_multiply_fusion
  553.4 32.2 %all-reduce.3.cloned.1.call-done = f32[128,128,128]{2,1,0:T(8,128)} async-done(((f32[128,128,128]{2,1,0:T(8,128)}), f32[128,128,128]{2,1,0:T(8,128)}) %all-reduce.3.cloned.1.call-update) | async-done | bytes 8388624 | tf_op jit(solution)/shard_map/psum | solution.py:69
  585.6 11.6 %multiply_reduce_fusion = (f32[128,128]{1,0:T(8,128)S(1)}, f32[128,128]{1,0:T(8,128)S(1)}) fusion(f32[128,128,128]{2,1,0:T(8,128)} %all-reduce.3.cloned.1.call-done, f32[128]{0:T(128)S(1)} %copy-done.10, f32[128,128]{1,0:T(8,128)S(1)} %add_rsqrt_fusion, f32[128,128]{1,0:T(8,128)S(1)} %broadcast_multiply_fusion.4, bf16[128,128,128]{2,1,0:T(8,128)(2,1)} %param.5), kind=kLoop, calls=%fused_computation.15 | loop fusion | flops 14647296 | bytes 12845568 | tf_op jit(solution)/shard_map/reduce_sum | solution.py:73
  597.2 0.0 copy-done.4
  597.2 0.0 copy-done.5
  597.2 10.7 %fusion.9 = bf16[128,128,128]{2,1,0:T(8,128)(2,1)} fusion(bf16[128,128,128]{2,1,0:T(8,128)(2,1)S(1)} %copy-done.4, f32[128,128,128]{2,1,0:T(8,128)S(1)} %copy-done.5, f32[128,128]{1,0:T(8,128)S(1)} %get-tuple-element.12, f32[128,128]{1,0:T(8,128)S(1)} %get-tuple-element.13, f32[128]{0:T(128)S(1)} %copy-done.10, f32[128,128]{1,0:T(8,128)S(1)} %add_rsqrt_fusion, ...), kind=kLoop, calls=%fused_computation.12 | loop fusion | flops 18874368 | bytes 17039872 | tf_op jit(solution)/shard_map/convert_element_type | solution.py:80
  (8 shorter events, 0.0 us)
Async XLA Ops:
  7.2 13.0 %copy-start = (bf16[4,128,64]{1,2,0:T(8,128)(2,1)S(1)}, bf16[4,128,64]{1,2,0:T(8,128)(2,1)}, u32[]{:S(2)}) copy-start(bf16[4,128,64]{1,2,0:T(8,128)(2,1)} %param.7) | copy-start | bytes 196612
  7.2 4.4 copy-start.11
  7.2 169.9 %all-gather.2.cloned.1.call-start = ((), (), s32[]{:S(2)}) async-start(), calls=%async_computation.1 | async-start | bytes 10485760 | tf_op jit(solution)/shard_map/all_gather | solution.py:32
  11.5 411.0 %reduce-scatter.2.cloned.1.call-start = ((), (), s32[]{:S(2)}) async-start(), calls=%async_computation.2 | async-start | bytes 20971520 | tf_op jit(solution)/shard_map/reduce_scatter | solution.py:56
  11.6 3.7 copy-start.2
  11.8 8.4 %copy-start.10 = (f32[128]{0:T(128)S(1)}, f32[128]{0:T(128)}, u32[]{:S(2)}) copy-start(f32[128]{0:T(128)} %param.6) | copy-start | bytes 1540
  24.9 5.9 copy-start.1
  32.1 48.9 %collective-permute-start = (bf16[128,64,128]{2,1,0:T(8,128)(2,1)S(1)}, bf16[128,64,128]{2,1,0:T(8,128)(2,1)S(1)}, u32[]{:S(2)}, u32[]{:S(2)}) collective-permute-start(bf16[128,64,128]{2,1,0:T(8,128)(2,1)S(1)} %multiply_convert_fusion.5), channel_id=1, source_target_pairs={{0,24},{8,0},{16,8},{24,16},{1,25},{9,1},{17,9},{25,17},{2,26},{10... | collective-permute-start | bytes 6291464 | tf_op jit(solution)/shard_map/ppermute | solution.py:45
  80.9 1.4 copy-start.6
  82.3 47.4 %collective-permute-start.1 = (bf16[128,64,128]{2,1,0:T(8,128)(2,1)S(1)}, bf16[128,64,128]{2,1,0:T(8,128)(2,1)}, u32[]{:S(2)}, u32[]{:S(2)}) collective-permute-start(bf16[128,64,128]{2,1,0:T(8,128)(2,1)S(1)} %collective-permute-done), channel_id=1, source_target_pairs={{0,24},{8,0},{16,8},{24,16},{1,25},{9,1},{17,9},{25,17},{2,26},{10... | collective-permute-start | bytes 6291464 | tf_op jit(solution)/shard_map/ppermute | solution.py:45
  129.7 47.4 %collective-permute-start.2 = (bf16[128,64,128]{2,1,0:T(8,128)(2,1)}, bf16[128,64,128]{2,1,0:T(8,128)(2,1)}, u32[]{:S(2)}, u32[]{:S(2)}) collective-permute-start(bf16[128,64,128]{2,1,0:T(8,128)(2,1)} %collective-permute-done.1), channel_id=1, source_target_pairs={{0,24},{8,0},{16,8},{24,16},{1,25},{9,1},{17,9},{25,17},{2,26},{10... | collective-permute-start | bytes 6291464 | tf_op jit(solution)/shard_map/ppermute | solution.py:45
  266.4 280.1 %all-reduce.5.cloned.1.call-start = ((), (), s32[]{:S(2)}) async-start(), calls=%async_computation.4 | async-start | bytes 262144 | tf_op jit(solution)/shard_map/psum | solution.py:76
  422.5 13.1 %copy-start.3 = (bf16[128,128,128]{2,1,0:T(8,128)(2,1)S(1)}, bf16[128,128,128]{2,1,0:T(8,128)(2,1)}, u32[]{:S(2)}) copy-start(bf16[128,128,128]{2,1,0:T(8,128)(2,1)} %param.5) | copy-start | bytes 12582916
  432.8 1.4 copy-start.7
  432.8 2.0 copy-start.8
  432.9 2.7 copy-start.9
  441.0 144.6 %all-reduce.3.cloned.1.call-start = ((), (), s32[]{:S(2)}) async-start(), calls=%async_computation.3 | async-start | bytes 16777216 | tf_op jit(solution)/shard_map/psum | solution.py:69
  585.6 11.6 %copy-start.4 = (bf16[128,128,128]{2,1,0:T(8,128)(2,1)S(1)}, bf16[128,128,128]{2,1,0:T(8,128)(2,1)}, u32[]{:S(2)}) copy-start(bf16[128,128,128]{2,1,0:T(8,128)(2,1)} %param.5) | copy-start | bytes 12582916
  585.6 11.6 %copy-start.5 = (f32[128,128,128]{2,1,0:T(8,128)S(1)}, f32[128,128,128]{2,1,0:T(8,128)}, u32[]{:S(2)}) copy-start(f32[128,128,128]{2,1,0:T(8,128)} %all-reduce.3.cloned.1.call-done) | copy-start | bytes 25165828
Sparse Core Ops, SparseCore 0:
  11.6 151.8 all-gather.1
  266.5 155.8 reduce-scatter.1
  441.1 105.3 all-reduce.4
  548.8 36.6 all-reduce.2
